TPU v7x, 32 devices: a whole 2x2x4 slice. The times are simulated.
32 devices in a mesh: section: 2 (over x), dp: 8 (over z, y), mp: 2 (over core).
Axes of the slice: x: 2, y: 2, z: 4, core: 2. Of those that a mesh axis runs over, the one named last changes fastest.
Arguments:
- layer_inputs: bfloat16 [2, 128, 4096], P('section', None, 'mp'), may hold values from -6 to 6
- pre_act: bfloat16 [2, 128, 8192], P('section', None, 'dp'), may hold values from -6 to 6
- out_grad: bfloat16 [128, 4096], P(None, 'mp'), may hold values from -4 to 4
- w_in: bfloat16 [8, 2, 512, 4096], P('dp', 'section', None, 'mp'), may hold values from -0.09375 to 0.09375
- w_out: bfloat16 [8, 2, 512, 4096], P('dp', 'section', None, 'mp'), may hold values from -0.0625 to 0.0625
Outputs:
- in_grads: bfloat16 [2, 128, 4096], P('section', None, 'mp')
- grad_in: float32 [8, 2, 512, 4096], P('dp', 'section', None, 'mp')
- grad_out: float32 [8, 2, 512, 4096], P('dp', 'section', None, 'mp')
All inputs are finite; a program needn't handle non-finite values.
Results may differ from a plain program's by a relative error of at most 0.035.
Values may be sent and summed in bfloat16 or wider, within the bound.
A program may use at most 64 MiB of HBM per device.

v0:
```python
import jax
import jax.numpy as jnp
from jax import lax
from jax.sharding import PartitionSpec as P

MICRO = 2


def shifted(value, axis, by):
    size = lax.axis_size(axis)
    pairs = [(i, i + by) for i in range(size) if 0 <= i + by < size]
    return lax.ppermute(value, axis, pairs)


def gelu_slope(value):
    cdf = 0.5 * (1.0 + lax.erf(value * 0.7071067811865476))
    dens = jnp.exp(-0.5 * value * value) * 0.3989422804014327
    return cdf + value * dens


def rounded(value):
    return lax.optimization_barrier(value.astype(jnp.bfloat16)).astype(jnp.float32)


def by_tokens(left, right):
    return lax.dot_general(
        left, right, (((0,), (0,)), ((), ())), preferred_element_type=jnp.float32
    )


def body(layer_inputs, pre_act, out_grad, w_in, w_out):
    sections = lax.axis_size("section")
    spot = lax.axis_index("section")
    tok_rows = out_grad.shape[0]
    block = tok_rows // MICRO
    width = out_grad.shape[1]
    full_in, full_out = (
        lax.all_gather(w_in, "section", axis=1, tiled=True),
        lax.all_gather(w_out, "section", axis=1, tiled=True),
    )
    units = full_in.shape[1] * full_in.shape[2]
    per_block = full_in.shape[2]
    in_rows = full_in.reshape(units, width)
    out_rows = full_out.reshape(units, width)
    inputs = layer_inputs[0]
    saved = pre_act[0]
    is_last = spot == sections - 1

    def advance(step, state):
        incoming, dys, gees, results = state
        micro_id = step - (sections - 1 - spot)
        valid = jnp.logical_and(micro_id >= 0, micro_id < MICRO)
        begin = jnp.clip(micro_id, 0, MICRO - 1) * block
        given = lax.dynamic_slice_in_dim(out_grad, begin, block, 0)
        upper = jnp.where(is_last, given, incoming)
        partial_value = lax.dot_general(
            upper, out_rows, (((1,), (1,)), ((), ())), preferred_element_type=jnp.float32
        )
        summed = lax.psum(partial_value.astype(jnp.bfloat16), "mp").astype(jnp.float32)
        rows_pre = lax.dynamic_slice_in_dim(saved, begin, block, 0).astype(jnp.float32)
        gee = (summed * gelu_slope(rows_pre)).astype(jnp.bfloat16)
        branch = jnp.dot(gee, in_rows, preferred_element_type=jnp.float32)
        total = lax.psum(branch.astype(jnp.bfloat16), "dp").astype(jnp.float32)
        result = (upper.astype(jnp.float32) + total).astype(jnp.bfloat16)
        outgoing = shifted(result, "section", -1)
        old_dy = lax.dynamic_slice_in_dim(dys, begin, block, 0)
        old_gee = lax.dynamic_slice_in_dim(gees, begin, block, 0)
        old_res = lax.dynamic_slice_in_dim(results, begin, block, 0)
        dys = lax.dynamic_update_slice_in_dim(dys, jnp.where(valid, upper, old_dy), begin, 0)
        gees = lax.dynamic_update_slice_in_dim(gees, jnp.where(valid, gee, old_gee), begin, 0)
        results = lax.dynamic_update_slice_in_dim(
            results, jnp.where(valid, result, old_res), begin, 0
        )
        return (outgoing, dys, gees, results)

    start_state = (
        jnp.zeros((block, width), jnp.bfloat16),
        jnp.zeros((tok_rows, width), jnp.bfloat16),
        jnp.zeros((tok_rows, units), jnp.bfloat16),
        jnp.zeros((tok_rows, width), jnp.bfloat16),
    )
    final_state = lax.fori_loop(0, sections + MICRO - 1, advance, start_state)
    dys = final_state[1]
    gees = final_state[2]
    results = final_state[3]
    hidden = jax.nn.gelu(saved.astype(jnp.float32), approximate=False).astype(jnp.bfloat16)
    offset = spot * per_block
    empty = jnp.zeros((per_block, width), jnp.float32)
    piece = (
        lax.all_gather(inputs[None], "section", axis=0, tiled=True),
        lax.all_gather(dys[None], "section", axis=0, tiled=True),
        lax.all_gather(gees[None], "section", axis=0, tiled=True),
        lax.all_gather(hidden[None], "section", axis=0, tiled=True),
    )
    acc_in = empty
    acc_out = empty
    for row in range(piece[0].shape[0]):
        gee_cols = lax.dynamic_slice_in_dim(piece[2][row], offset, per_block, 1)
        hid_cols = lax.dynamic_slice_in_dim(piece[3][row], offset, per_block, 1)
        acc_in = acc_in + rounded(by_tokens(gee_cols, piece[0][row]))
        acc_out = acc_out + rounded(by_tokens(hid_cols, piece[1][row]))
    acc_in, acc_out = (acc_in, acc_out)
    grad_in = acc_in.reshape(1, 1, per_block, width)
    grad_out = acc_out.reshape(1, 1, per_block, width)
    return (results[None], grad_in, grad_out)


def solution(mesh):
    in_specs = (
        P("section", None, "mp"),
        P("section", None, "dp"),
        P(None, "mp"),
        P("dp", "section", None, "mp"),
        P("dp", "section", None, "mp"),
    )
    out_specs = (
        P("section", None, "mp"),
        P("dp", "section", None, "mp"),
        P("dp", "section", None, "mp"),
    )
    return jax.shard_map(body, mesh=mesh, in_specs=in_specs, out_specs=out_specs, check_vma=False)
```

profile of v0, /device:TPU:0, one launch (start us, length us, event | category | flops | bytes accessed | tf_op | source)
XLA Modules:
  0.0 509.6 jit_solution(17135875296356808804)
XLA Ops:
  8.7 60.3 %all-gather.7.cloned.1.call-done = bf16[1,2,512,2048]{3,2,0,1:T(8,128)(2,1)} async-done(((bf16[1,1,512,2048]{3,2,0,1:T(8,128)(2,1)}), bf16[1,2,512,2048]{3,2,0,1:T(8,128)(2,1)}) %all-gather.7.cloned.1.call-update) | async-done | bytes 4194320 | tf_op jit(solution)/shard_map/all_gather | solution.py:39
  69.0 58.3 %all-gather.9.cloned.1.call-done = bf16[1,2,512,2048]{3,2,0,1:T(8,128)(2,1)} async-done(((bf16[1,1,512,2048]{3,2,0,1:T(8,128)(2,1)}), bf16[1,2,512,2048]{3,2,0,1:T(8,128)(2,1)}) %all-gather.9.cloned.1.call-update) | async-done | bytes 4194320 | tf_op jit(solution)/shard_map/all_gather | solution.py:38
  127.5 320.8 %while.21 = (s32[]{:T(128)}, bf16[64,2048]{1,0:T(8,128)(2,1)S(1)}, bf16[128,2048]{1,0:T(8,128)(2,1)S(1)}, bf16[128,1024]{1,0:T(8,128)(2,1)S(1)}, bf16[128,2048]{...) while((s32[]{:T(128)}, bf16[64,2048]{1,0:T(8,128)(2,1)S(1)}, ...), condition=%wide.region_3.4_spmd, body=%wide.region_0.3_spmd.sunk | while | flops 539820032 | bytes 16384420 | solution.py:82
  127.7 4.2 convolution_convert_fusion.8
  132.0 18.0 %all-reduce.3.cloned.1.call-done = bf16[64,1024]{1,0:T(8,128)(2,1)} async-done(((bf16[64,1024]{1,0:T(8,128)(2,1)}), bf16[64,1024]{1,0:T(8,128)(2,1)}) %all-reduce.3.cloned.1.call-update) | async-done | bytes 131088 | tf_op jit(solution)/shard_map/while/body/eval_jaxpr/psum | solution.py:59
  150.0 3.9 convolution_convert_fusion.9
  153.9 72.4 %all-reduce.5.cloned.1.call-done = bf16[64,2048]{1,0:T(8,128)(2,1)} async-done(((bf16[64,2048]{1,0:T(8,128)(2,1)}), bf16[64,2048]{1,0:T(8,128)(2,1)}) %all-reduce.5.cloned.1.call-update) | async-done | bytes 262160 | tf_op jit(solution)/shard_map/while/body/eval_jaxpr/psum | solution.py:63
  227.3 1.3 collective-permute-start
  228.8 6.8 %collective-permute-done = bf16[64,2048]{1,0:T(8,128)(2,1)S(1)} collective-permute-done((bf16[64,2048]{1,0:T(8,128)(2,1)S(1)}, bf16[64,2048]{1,0:T(8,128)(2,1)S(1)}, u32[]{:S(2)}, u32[]{:S(2)}) %collective-permute-start) | collective-permute-done | bytes 262176 | tf_op jit(solution)/shard_map/while/body/eval_jaxpr/ppermute | solution.py:12
  235.7 4.2 convolution_convert_fusion.8
  240.1 16.3 %all-reduce.3.cloned.1.call-done = bf16[64,1024]{1,0:T(8,128)(2,1)} async-done(((bf16[64,1024]{1,0:T(8,128)(2,1)}), bf16[64,1024]{1,0:T(8,128)(2,1)}) %all-reduce.3.cloned.1.call-update) | async-done | bytes 131088 | tf_op jit(solution)/shard_map/while/body/eval_jaxpr/psum | solution.py:59
  256.4 3.9 convolution_convert_fusion.9
  260.3 72.4 %all-reduce.5.cloned.1.call-done = bf16[64,2048]{1,0:T(8,128)(2,1)} async-done(((bf16[64,2048]{1,0:T(8,128)(2,1)}), bf16[64,2048]{1,0:T(8,128)(2,1)}) %all-reduce.5.cloned.1.call-update) | async-done | bytes 262160 | tf_op jit(solution)/shard_map/while/body/eval_jaxpr/psum | solution.py:63
  333.7 1.3 collective-permute-start
  335.2 6.8 %collective-permute-done = bf16[64,2048]{1,0:T(8,128)(2,1)S(1)} collective-permute-done((bf16[64,2048]{1,0:T(8,128)(2,1)S(1)}, bf16[64,2048]{1,0:T(8,128)(2,1)S(1)}, u32[]{:S(2)}, u32[]{:S(2)}) %collective-permute-start) | collective-permute-done | bytes 262176 | tf_op jit(solution)/shard_map/while/body/eval_jaxpr/ppermute | solution.py:12
  342.1 4.2 convolution_convert_fusion.8
  346.4 16.3 %all-reduce.3.cloned.1.call-done = bf16[64,1024]{1,0:T(8,128)(2,1)} async-done(((bf16[64,1024]{1,0:T(8,128)(2,1)}), bf16[64,1024]{1,0:T(8,128)(2,1)}) %all-reduce.3.cloned.1.call-update) | async-done | bytes 131088 | tf_op jit(solution)/shard_map/while/body/eval_jaxpr/psum | solution.py:59
  362.7 3.9 convolution_convert_fusion.9
  366.6 72.4 %all-reduce.5.cloned.1.call-done = bf16[64,2048]{1,0:T(8,128)(2,1)} async-done(((bf16[64,2048]{1,0:T(8,128)(2,1)}), bf16[64,2048]{1,0:T(8,128)(2,1)}) %all-reduce.5.cloned.1.call-update) | async-done | bytes 262160 | tf_op jit(solution)/shard_map/while/body/eval_jaxpr/psum | solution.py:63
  440.1 1.3 collective-permute-start
  441.5 6.8 %collective-permute-done = bf16[64,2048]{1,0:T(8,128)(2,1)S(1)} collective-permute-done((bf16[64,2048]{1,0:T(8,128)(2,1)S(1)}, bf16[64,2048]{1,0:T(8,128)(2,1)S(1)}, u32[]{:S(2)}, u32[]{:S(2)}) %collective-permute-start) | collective-permute-done | bytes 262176 | tf_op jit(solution)/shard_map/while/body/eval_jaxpr/ppermute | solution.py:12
  449.1 1.1 fusion.10
  450.2 8.1 %all_gather.22 = bf16[2,128,1024]{2,1,0:T(8,128)(2,1)S(1)} all-gather(bf16[1,128,1024]{2,1,0:T(8,128)(2,1)S(1)} %fusion.10), channel_id=1, replica_groups=mesh['section'=2,'dp'=8,'mp'=2] {'section'}, dimensions={0}, use_global_device_ids=true | all-gather | bytes 786432 | tf_op jit(solution)/shard_map/all_gather | solution.py:93
  458.3 12.7 %all-gather = bf16[256,1024]{1,0:T(8,128)(2,1)S(1)} all-gather(bf16[128,1024]{1,0:T(8,128)(2,1)S(1)} %get-tuple-element.260), channel_id=2, replica_groups=mesh['section'=2,'dp'=8,'mp'=2] {'section'}, dimensions={0}, use_global_device_ids=true | all-gather | bytes 786432 | tf_op jit(solution)/shard_map/all_gather | solution.py:92
  471.1 3.3 all-gather.11.cloned.1.call-done
  474.4 1.8 convolution_convert_fusion.4
  476.2 1.8 convolution_convert_fusion.5
  478.0 2.8 add_bitcast_fusion.1
  480.8 15.6 %all-gather.13.cloned.1.call-done = bf16[256,2048]{1,0:T(8,128)(2,1)} async-done(((bf16[128,2048]{1,0:T(8,128)(2,1)}), bf16[256,2048]{1,0:T(8,128)(2,1)}) %all-gather.13.cloned.1.call-update) | async-done | bytes 1048592 | tf_op jit(solution)/shard_map/all_gather | solution.py:91
  496.4 1.8 convolution_convert_fusion.2
  498.1 1.8 convolution_convert_fusion.3
  499.9 2.8 add_bitcast_fusion
  (49 shorter events, 6.7 us)
Async XLA Ops:
  7.2 120.3 %copy-start.4 = (bf16[128,2048]{1,0:T(8,128)(2,1)S(1)}, bf16[128,2048]{1,0:T(8,128)(2,1)}, u32[]{:S(2)}) copy-start(bf16[128,2048]{1,0:T(8,128)(2,1)} %param.9) | copy-start | bytes 1572868
  7.2 120.3 %copy-start.2 = (bf16[1,128,1024]{2,1,0:T(8,128)(2,1)S(1)}, bf16[1,128,1024]{2,1,0:T(8,128)(2,1)}, u32[]{:S(2)}) copy-start(bf16[1,128,1024]{2,1,0:T(8,128)(2,1)} %param.8) | copy-start | bytes 786436
  7.2 61.8 %all-gather.7.cloned.1.call-start = ((), (), s32[]{:S(2)}) async-start(), calls=%async_computation | async-start | bytes 6291456 | tf_op jit(solution)/shard_map/all_gather | solution.py:39
  7.9 119.4 %all-gather.9.cloned.1.call-start = ((), (), s32[]{:S(2)}) async-start(), calls=%async_computation.1 | async-start | bytes 6291456 | tf_op jit(solution)/shard_map/all_gather | solution.py:38
  127.5 22.5 %all-reduce.3.cloned.1.call-start = ((), (), s32[]{:S(2)}) async-start(), calls=%async_computation.4 | async-start | bytes 262144 | tf_op jit(solution)/shard_map/while/body/eval_jaxpr/psum | solution.py:59
  132.0 94.3 %all-reduce.5.cloned.1.call-start = ((), (), s32[]{:S(2)}) async-start(), calls=%async_computation.5 | async-start | bytes 524288 | tf_op jit(solution)/shard_map/while/body/eval_jaxpr/psum | solution.py:63
  150.0 78.6 %copy-start = (bf16[64,1024]{1,0:T(8,128)(2,1)S(1)}, bf16[64,1024]{1,0:T(8,128)(2,1)}, u32[]{:S(2)}) copy-start(bf16[64,1024]{1,0:T(8,128)(2,1)} %all-reduce.3.cloned.1.call-done) | copy-start | bytes 393220 | tf_op jit(solution)/shard_map/while
  227.3 8.3 %collective-permute-start = (bf16[64,2048]{1,0:T(8,128)(2,1)S(1)}, bf16[64,2048]{1,0:T(8,128)(2,1)S(1)}, u32[]{:S(2)}, u32[]{:S(2)}) collective-permute-start(bf16[64,2048]{1,0:T(8,128)(2,1)S(1)} %get-tuple-element.364), channel_id=1, source_target_pairs={{16,0},{17,1},{18,2},{19,3},{20,4},{21,5},{22,6},{23,7},{24,8},{25... | collective-permute-start | bytes 786440 | tf_op jit(solution)/shard_map/while/body/eval_jaxpr/ppermute | solution.py:12
  235.6 20.8 %all-reduce.3.cloned.1.call-start = ((), (), s32[]{:S(2)}) async-start(), calls=%async_computation.4 | async-start | bytes 262144 | tf_op jit(solution)/shard_map/while/body/eval_jaxpr/psum | solution.py:59
  240.0 92.6 %all-reduce.5.cloned.1.call-start = ((), (), s32[]{:S(2)}) async-start(), calls=%async_computation.5 | async-start | bytes 524288 | tf_op jit(solution)/shard_map/while/body/eval_jaxpr/psum | solution.py:63
  256.4 78.6 %copy-start = (bf16[64,1024]{1,0:T(8,128)(2,1)S(1)}, bf16[64,1024]{1,0:T(8,128)(2,1)}, u32[]{:S(2)}) copy-start(bf16[64,1024]{1,0:T(8,128)(2,1)} %all-reduce.3.cloned.1.call-done) | copy-start | bytes 393220 | tf_op jit(solution)/shard_map/while
  333.7 8.3 %collective-permute-start = (bf16[64,2048]{1,0:T(8,128)(2,1)S(1)}, bf16[64,2048]{1,0:T(8,128)(2,1)S(1)}, u32[]{:S(2)}, u32[]{:S(2)}) collective-permute-start(bf16[64,2048]{1,0:T(8,128)(2,1)S(1)} %get-tuple-element.364), channel_id=1, source_target_pairs={{16,0},{17,1},{18,2},{19,3},{20,4},{21,5},{22,6},{23,7},{24,8},{25... | collective-permute-start | bytes 786440 | tf_op jit(solution)/shard_map/while/body/eval_jaxpr/ppermute | solution.py:12
  342.0 20.8 %all-reduce.3.cloned.1.call-start = ((), (), s32[]{:S(2)}) async-start(), calls=%async_computation.4 | async-start | bytes 262144 | tf_op jit(solution)/shard_map/while/body/eval_jaxpr/psum | solution.py:59
  346.4 92.6 %all-reduce.5.cloned.1.call-start = ((), (), s32[]{:S(2)}) async-start(), calls=%async_computation.5 | async-start | bytes 524288 | tf_op jit(solution)/shard_map/while/body/eval_jaxpr/psum | solution.py:63
  362.7 78.6 %copy-start = (bf16[64,1024]{1,0:T(8,128)(2,1)S(1)}, bf16[64,1024]{1,0:T(8,128)(2,1)}, u32[]{:S(2)}) copy-start(bf16[64,1024]{1,0:T(8,128)(2,1)} %all-reduce.3.cloned.1.call-done) | copy-start | bytes 393220 | tf_op jit(solution)/shard_map/while
  440.1 8.3 %collective-permute-start = (bf16[64,2048]{1,0:T(8,128)(2,1)S(1)}, bf16[64,2048]{1,0:T(8,128)(2,1)S(1)}, u32[]{:S(2)}, u32[]{:S(2)}) collective-permute-start(bf16[64,2048]{1,0:T(8,128)(2,1)S(1)} %get-tuple-element.364), channel_id=1, source_target_pairs={{16,0},{17,1},{18,2},{19,3},{20,4},{21,5},{22,6},{23,7},{24,8},{25... | collective-permute-start | bytes 786440 | tf_op jit(solution)/shard_map/while/body/eval_jaxpr/ppermute | solution.py:12
  448.3 22.7 %copy-start.1 = (bf16[128,2048]{1,0:T(8,128)(2,1)}, bf16[128,2048]{1,0:T(8,128)(2,1)S(1)}, u32[]{:S(2)}) copy-start(bf16[128,2048]{1,0:T(8,128)(2,1)S(1)} %get-tuple-element.261) | copy-start | bytes 1572868
  448.3 29.6 %copy-start.3 = (bf16[128,2048]{1,0:T(8,128)(2,1)}, bf16[128,2048]{1,0:T(8,128)(2,1)S(1)}, u32[]{:S(2)}) copy-start(bf16[128,2048]{1,0:T(8,128)(2,1)S(1)} %get-tuple-element.259) | copy-start | bytes 1572868
  448.3 26.1 %all-gather.11.cloned.1.call-start = ((), (), s32[]{:S(2)}) async-start(), calls=%async_computation.2 | async-start | bytes 1572864 | tf_op jit(solution)/shard_map/all_gather | solution.py:90
  449.1 47.3 %all-gather.13.cloned.1.call-start = ((), (), s32[]{:S(2)}) async-start(), calls=%async_computation.3 | async-start | bytes 1572864 | tf_op jit(solution)/shard_map/all_gather | solution.py:91
Sparse Core Ops, SparseCore 0:
  9.5 59.4 all-gather.6
  70.6 56.7 all-gather.8
  132.1 17.8 all-reduce.2
  154.0 72.1 all-reduce.4
  240.1 16.1 all-reduce.2
  260.4 72.2 all-reduce.4
  346.5 16.1 all-reduce.2
  366.7 72.2 all-reduce.4
  450.7 23.6 all-gather.10
  476.4 19.9 all-gather.12
where the time goes:
time: 510 us
  waiting for transfers between devices  428 us (84%)
  matrix products  31.4 us (6%)
  blocking collectives  20.7 us (4%)
  between operations  14.2 us (3%)
  other arithmetic  10.8 us (2%)
    psum x3, waiting for transfers between devices, advance(): total = lax.psum(branch.astype(jnp.bfloat16), 'dp').astype(jnp.float32)  217 us
    all_gather x1, waiting for transfers between devices, body(): lax.all_gather(w_out, 'section', axis=1, tiled=True)  60.3 us
    all_gather x1, waiting for transfers between devices, body(): lax.all_gather(w_in, 'section', axis=1, tiled=True)  58.3 us
    psum x3, waiting for transfers between devices, advance(): lax.psum(partial_value.astype(jnp.bfloat16), 'mp').astype(jnp.float32)  50.6 us
    ppermute x3, waiting for transfers between devices, shifted(): return lax.ppermute(value, axis, pairs)  20.4 us
    all_gather x1, waiting for transfers between devices, body(): lax.all_gather(dys[None], 'section', axis=0, tiled=True)  15.6 us
    dot_general x3, matrix products, advance(): lax.dot_general(upper, out_rows, (((1,), (1,)), ((), ())), preferred_elem...  12.7 us
    all_gather x1, blocking collectives, body(): lax.all_gather(gees[None], 'section', axis=0, tiled=True)  12.7 us
  transfers between devices with their start and end apart: 13, of which 13 were waited for; matrix products, arithmetic and copies ran while one was open for 2% of the time, Pallas kernels for 0%

commit v1 on v0

--- a/solution.py
+++ b/solution.py
@@ -4,6 +4,11 @@
 from jax.sharding import PartitionSpec as P
 
 MICRO = 2
+
+
+def gather_by_exchange(value, axis, dim):
+    copies = jnp.concatenate([value] * lax.axis_size(axis), axis=dim)
+    return lax.all_to_all(copies, axis, dim, dim, tiled=True)
 
 
 def shifted(value, axis, by):
@@ -36,7 +41,7 @@
     width = out_grad.shape[1]
     full_in, full_out = (
         lax.all_gather(w_in, "section", axis=1, tiled=True),
-        lax.all_gather(w_out, "section", axis=1, tiled=True),
+        gather_by_exchange(w_out, "section", 1),
     )
     units = full_in.shape[1] * full_in.shape[2]
     per_block = full_in.shape[2]

time: 510 us -> 496 us (0.973)
  waiting for transfers between devices: 428 us -> 403 us
  starting transfers between devices: 4.17 us -> 9.86 us
    all_to_all x0 -> x1, waiting for transfers between devices: none -> 92.9 us  [gather_by_exchange(): return lax.all_to_all(copies, axis, dim, dim, tiled=True)]
    all_gather x1 -> x0, waiting for transfers between devices: 60.3 us -> none  [body(): lax.all_gather(w_out, 'section', axis=1, tiled=True)]
    all_gather x1, waiting for transfers between devices: 58.3 us -> 1.07 us  [body(): lax.all_gather(w_in, 'section', axis=1, tiled=True)]
    all_to_all x0 -> x1, starting transfers between devices: none -> 5.73 us  [gather_by_exchange(): return lax.all_to_all(copies, axis, dim, dim, tiled=True)]
  transfers between devices with their start and end apart: 13 -> 13, of which waited for: 13 -> 13; matrix products, arithmetic and copies ran while one was open for 2% -> 3% of each run, Pallas kernels for 0% -> 0%
where the time goes in v1:
time: 496 us; the launch traced here: 495 us
  waiting for transfers between devices  403 us (81%)
  matrix products  31.4 us (6%)
  blocking collectives  20.7 us (4%)
  other arithmetic  15.4 us (3%)
  between operations  13.9 us (3%)
  starting transfers between devices  9.86 us (2%)
    psum x3, waiting for transfers between devices, advance(): total = lax.psum(branch.astype(jnp.bfloat16), 'dp').astype(jnp.float32)  217 us
    all_to_all x1, waiting for transfers between devices, gather_by_exchange(): return lax.all_to_all(copies, axis, dim, dim, tiled=True)  92.9 us
    psum x3, waiting for transfers between devices, advance(): lax.psum(partial_value.astype(jnp.bfloat16), 'mp').astype(jnp.float32)  51.2 us
    ppermute x3, waiting for transfers between devices, shifted(): return lax.ppermute(value, axis, pairs)  20.4 us
    all_gather x1, waiting for transfers between devices, body(): lax.all_gather(dys[None], 'section', axis=0, tiled=True)  15.7 us
    dot_general x3, matrix products, advance(): lax.dot_general(upper, out_rows, (((1,), (1,)), ((), ())), preferred_elem...  12.7 us
    all_gather x1, blocking collectives, body(): lax.all_gather(gees[None], 'section', axis=0, tiled=True)  12.7 us
    dot_general x3, matrix products, advance(): branch = jnp.dot(gee, in_rows, preferred_element_type=jnp.float32)  11.6 us
  transfers between devices with their start and end apart: 13, of which 13 were waited for; matrix products, arithmetic and copies ran while one was open for 3% of the time, Pallas kernels for 0%

profile of v1, /device:TPU:0, one launch (start us, length us, event | category | flops | bytes accessed | tf_op | source)
XLA Modules:
  0.0 494.9 jit_solution(4044905733619837821)
XLA Ops:
  7.9 4.6 pad_maximum_fusion
  12.5 5.7 %all-to-all-start = ((bf16[1,2,512,2048]{3,2,0,1:T(8,128)(2,1)}), bf16[1,2,512,2048]{3,2,0,1:T(8,128)(2,1)}, u32[]{:S(2)}, u32[]{:S(2)}) async-start(bf16[1,2,512,2048]{3,2,0,1:T(8,128)(2,1)} %pad_maximum_fusion), calls=%async_computation | async-start | bytes 8388608 | tf_op jit(solution)/shard_map/all_to_all | solution.py:11
  18.3 92.9 %all-to-all-done = bf16[1,2,512,2048]{3,2,0,1:T(8,128)(2,1)} async-done(((bf16[1,2,512,2048]{3,2,0,1:T(8,128)(2,1)}), bf16[1,2,512,2048]{3,2,0,1:T(8,128)(2,1)}, u32[]{:S(2)}, u32[]{:S(2)}) %all-to-all-start) | async-done | bytes 4194336 | tf_op jit(solution)/shard_map/all_to_all | solution.py:11
  112.4 321.4 %while.21 = (s32[]{:T(128)}, bf16[64,2048]{1,0:T(8,128)(2,1)S(1)}, bf16[128,2048]{1,0:T(8,128)(2,1)S(1)}, bf16[128,1024]{1,0:T(8,128)(2,1)S(1)}, bf16[128,2048]{...) while((s32[]{:T(128)}, bf16[64,2048]{1,0:T(8,128)(2,1)S(1)}, ...), condition=%wide.region_3.4_spmd, body=%wide.region_0.3_spmd.sunk | while | flops 539820032 | bytes 16384420 | solution.py:87
  112.6 4.2 convolution_convert_fusion.8
  116.9 18.6 %all-reduce.3.cloned.1.call-done = bf16[64,1024]{1,0:T(8,128)(2,1)} async-done(((bf16[64,1024]{1,0:T(8,128)(2,1)}), bf16[64,1024]{1,0:T(8,128)(2,1)}) %all-reduce.3.cloned.1.call-update) | async-done | bytes 131088 | tf_op jit(solution)/shard_map/while/body/eval_jaxpr/psum | solution.py:64
  135.5 3.9 convolution_convert_fusion.9
  139.4 72.4 %all-reduce.5.cloned.1.call-done = bf16[64,2048]{1,0:T(8,128)(2,1)} async-done(((bf16[64,2048]{1,0:T(8,128)(2,1)}), bf16[64,2048]{1,0:T(8,128)(2,1)}) %all-reduce.5.cloned.1.call-update) | async-done | bytes 262160 | tf_op jit(solution)/shard_map/while/body/eval_jaxpr/psum | solution.py:68
  212.9 1.3 collective-permute-start
  214.3 6.8 %collective-permute-done = bf16[64,2048]{1,0:T(8,128)(2,1)S(1)} collective-permute-done((bf16[64,2048]{1,0:T(8,128)(2,1)S(1)}, bf16[64,2048]{1,0:T(8,128)(2,1)S(1)}, u32[]{:S(2)}, u32[]{:S(2)}) %collective-permute-start) | collective-permute-done | bytes 262176 | tf_op jit(solution)/shard_map/while/body/eval_jaxpr/ppermute | solution.py:17
  221.3 4.2 convolution_convert_fusion.8
  225.6 16.3 %all-reduce.3.cloned.1.call-done = bf16[64,1024]{1,0:T(8,128)(2,1)} async-done(((bf16[64,1024]{1,0:T(8,128)(2,1)}), bf16[64,1024]{1,0:T(8,128)(2,1)}) %all-reduce.3.cloned.1.call-update) | async-done | bytes 131088 | tf_op jit(solution)/shard_map/while/body/eval_jaxpr/psum | solution.py:64
  241.9 3.9 convolution_convert_fusion.9
  245.8 72.4 %all-reduce.5.cloned.1.call-done = bf16[64,2048]{1,0:T(8,128)(2,1)} async-done(((bf16[64,2048]{1,0:T(8,128)(2,1)}), bf16[64,2048]{1,0:T(8,128)(2,1)}) %all-reduce.5.cloned.1.call-update) | async-done | bytes 262160 | tf_op jit(solution)/shard_map/while/body/eval_jaxpr/psum | solution.py:68
  319.2 1.3 collective-permute-start
  320.7 6.8 %collective-permute-done = bf16[64,2048]{1,0:T(8,128)(2,1)S(1)} collective-permute-done((bf16[64,2048]{1,0:T(8,128)(2,1)S(1)}, bf16[64,2048]{1,0:T(8,128)(2,1)S(1)}, u32[]{:S(2)}, u32[]{:S(2)}) %collective-permute-start) | collective-permute-done | bytes 262176 | tf_op jit(solution)/shard_map/while/body/eval_jaxpr/ppermute | solution.py:17
  327.6 4.2 convolution_convert_fusion.8
  331.9 16.3 %all-reduce.3.cloned.1.call-done = bf16[64,1024]{1,0:T(8,128)(2,1)} async-done(((bf16[64,1024]{1,0:T(8,128)(2,1)}), bf16[64,1024]{1,0:T(8,128)(2,1)}) %all-reduce.3.cloned.1.call-update) | async-done | bytes 131088 | tf_op jit(solution)/shard_map/while/body/eval_jaxpr/psum | solution.py:64
  348.2 3.9 convolution_convert_fusion.9
  352.1 72.4 %all-reduce.5.cloned.1.call-done = bf16[64,2048]{1,0:T(8,128)(2,1)} async-done(((bf16[64,2048]{1,0:T(8,128)(2,1)}), bf16[64,2048]{1,0:T(8,128)(2,1)}) %all-reduce.5.cloned.1.call-update) | async-done | bytes 262160 | tf_op jit(solution)/shard_map/while/body/eval_jaxpr/psum | solution.py:68
  425.5 1.3 collective-permute-start
  427.0 6.8 %collective-permute-done = bf16[64,2048]{1,0:T(8,128)(2,1)S(1)} collective-permute-done((bf16[64,2048]{1,0:T(8,128)(2,1)S(1)}, bf16[64,2048]{1,0:T(8,128)(2,1)S(1)}, u32[]{:S(2)}, u32[]{:S(2)}) %collective-permute-start) | collective-permute-done | bytes 262176 | tf_op jit(solution)/shard_map/while/body/eval_jaxpr/ppermute | solution.py:17
  435.7 8.1 %all_gather.18 = bf16[2,128,1024]{2,1,0:T(8,128)(2,1)S(1)} all-gather(bf16[1,128,1024]{2,1,0:T(8,128)(2,1)S(1)} %fusion.10), channel_id=1, replica_groups=mesh['section'=2,'dp'=8,'mp'=2] {'section'}, dimensions={0}, use_global_device_ids=true | all-gather | bytes 786432 | tf_op jit(solution)/shard_map/all_gather | solution.py:98
  443.8 12.7 %all-gather = bf16[256,1024]{1,0:T(8,128)(2,1)S(1)} all-gather(bf16[128,1024]{1,0:T(8,128)(2,1)S(1)} %get-tuple-element.260), channel_id=2, replica_groups=mesh['section'=2,'dp'=8,'mp'=2] {'section'}, dimensions={0}, use_global_device_ids=true | all-gather | bytes 786432 | tf_op jit(solution)/shard_map/all_gather | solution.py:97
  456.6 3.3 all-gather.8.cloned.1.call-done
  459.9 1.8 convolution_convert_fusion.4
  461.6 1.8 convolution_convert_fusion.5
  463.4 2.8 add_bitcast_fusion.1
  466.2 15.7 %all-gather.10.cloned.1.call-done = bf16[256,2048]{1,0:T(8,128)(2,1)} async-done(((bf16[128,2048]{1,0:T(8,128)(2,1)}), bf16[256,2048]{1,0:T(8,128)(2,1)}) %all-gather.10.cloned.1.call-update) | async-done | bytes 1048592 | tf_op jit(solution)/shard_map/all_gather | solution.py:96
  482.0 1.8 convolution_convert_fusion.2
  483.8 1.8 convolution_convert_fusion.3
  485.5 2.8 add_bitcast_fusion
  (49 shorter events, 8.2 us)
Async XLA Ops:
  7.2 105.0 %all-gather.6.cloned.1.call-start = ((), (), s32[]{:S(2)}) async-start(), calls=%async_computation.1 | async-start | bytes 6291456 | tf_op jit(solution)/shard_map/all_gather | solution.py:43
  12.5 99.9 %copy-start.2 = (bf16[1,128,1024]{2,1,0:T(8,128)(2,1)S(1)}, bf16[1,128,1024]{2,1,0:T(8,128)(2,1)}, u32[]{:S(2)}) copy-start(bf16[1,128,1024]{2,1,0:T(8,128)(2,1)} %param.8) | copy-start | bytes 786436
  12.5 99.9 %copy-start.4 = (bf16[128,2048]{1,0:T(8,128)(2,1)S(1)}, bf16[128,2048]{1,0:T(8,128)(2,1)}, u32[]{:S(2)}) copy-start(bf16[128,2048]{1,0:T(8,128)(2,1)} %param.9) | copy-start | bytes 1572868
  12.5 98.6 %all-to-all-start = ((bf16[1,2,512,2048]{3,2,0,1:T(8,128)(2,1)}), bf16[1,2,512,2048]{3,2,0,1:T(8,128)(2,1)}, u32[]{:S(2)}, u32[]{:S(2)}) async-start(bf16[1,2,512,2048]{3,2,0,1:T(8,128)(2,1)} %pad_maximum_fusion), calls=%async_computation | async-start | bytes 8388608 | tf_op jit(solution)/shard_map/all_to_all | solution.py:11
  112.4 23.1 %all-reduce.3.cloned.1.call-start = ((), (), s32[]{:S(2)}) async-start(), calls=%async_computation.4 | async-start | bytes 262144 | tf_op jit(solution)/shard_map/while/body/eval_jaxpr/psum | solution.py:64
  116.9 94.9 %all-reduce.5.cloned.1.call-start = ((), (), s32[]{:S(2)}) async-start(), calls=%async_computation.5 | async-start | bytes 524288 | tf_op jit(solution)/shard_map/while/body/eval_jaxpr/psum | solution.py:68
  135.5 78.6 %copy-start = (bf16[64,1024]{1,0:T(8,128)(2,1)S(1)}, bf16[64,1024]{1,0:T(8,128)(2,1)}, u32[]{:S(2)}) copy-start(bf16[64,1024]{1,0:T(8,128)(2,1)} %all-reduce.3.cloned.1.call-done) | copy-start | bytes 393220 | tf_op jit(solution)/shard_map/while
  212.9 8.3 %collective-permute-start = (bf16[64,2048]{1,0:T(8,128)(2,1)S(1)}, bf16[64,2048]{1,0:T(8,128)(2,1)S(1)}, u32[]{:S(2)}, u32[]{:S(2)}) collective-permute-start(bf16[64,2048]{1,0:T(8,128)(2,1)S(1)} %get-tuple-element.364), channel_id=1, source_target_pairs={{16,0},{17,1},{18,2},{19,3},{20,4},{21,5},{22,6},{23,7},{24,8},{25... | collective-permute-start | bytes 786440 | tf_op jit(solution)/shard_map/while/body/eval_jaxpr/ppermute | solution.py:17
  221.1 20.8 %all-reduce.3.cloned.1.call-start = ((), (), s32[]{:S(2)}) async-start(), calls=%async_computation.4 | async-start | bytes 262144 | tf_op jit(solution)/shard_map/while/body/eval_jaxpr/psum | solution.py:64
  225.5 92.6 %all-reduce.5.cloned.1.call-start = ((), (), s32[]{:S(2)}) async-start(), calls=%async_computation.5 | async-start | bytes 524288 | tf_op jit(solution)/shard_map/while/body/eval_jaxpr/psum | solution.py:68
  241.9 78.6 %copy-start = (bf16[64,1024]{1,0:T(8,128)(2,1)S(1)}, bf16[64,1024]{1,0:T(8,128)(2,1)}, u32[]{:S(2)}) copy-start(bf16[64,1024]{1,0:T(8,128)(2,1)} %all-reduce.3.cloned.1.call-done) | copy-start | bytes 393220 | tf_op jit(solution)/shard_map/while
  319.2 8.3 %collective-permute-start = (bf16[64,2048]{1,0:T(8,128)(2,1)S(1)}, bf16[64,2048]{1,0:T(8,128)(2,1)S(1)}, u32[]{:S(2)}, u32[]{:S(2)}) collective-permute-start(bf16[64,2048]{1,0:T(8,128)(2,1)S(1)} %get-tuple-element.364), channel_id=1, source_target_pairs={{16,0},{17,1},{18,2},{19,3},{20,4},{21,5},{22,6},{23,7},{24,8},{25... | collective-permute-start | bytes 786440 | tf_op jit(solution)/shard_map/while/body/eval_jaxpr/ppermute | solution.py:17
  327.5 20.8 %all-reduce.3.cloned.1.call-start = ((), (), s32[]{:S(2)}) async-start(), calls=%async_computation.4 | async-start | bytes 262144 | tf_op jit(solution)/shard_map/while/body/eval_jaxpr/psum | solution.py:64
  331.9 92.6 %all-reduce.5.cloned.1.call-start = ((), (), s32[]{:S(2)}) async-start(), calls=%async_computation.5 | async-start | bytes 524288 | tf_op jit(solution)/shard_map/while/body/eval_jaxpr/psum | solution.py:68
  348.2 78.6 %copy-start = (bf16[64,1024]{1,0:T(8,128)(2,1)S(1)}, bf16[64,1024]{1,0:T(8,128)(2,1)}, u32[]{:S(2)}) copy-start(bf16[64,1024]{1,0:T(8,128)(2,1)} %all-reduce.3.cloned.1.call-done) | copy-start | bytes 393220 | tf_op jit(solution)/shard_map/while
  425.5 8.3 %collective-permute-start = (bf16[64,2048]{1,0:T(8,128)(2,1)S(1)}, bf16[64,2048]{1,0:T(8,128)(2,1)S(1)}, u32[]{:S(2)}, u32[]{:S(2)}) collective-permute-start(bf16[64,2048]{1,0:T(8,128)(2,1)S(1)} %get-tuple-element.364), channel_id=1, source_target_pairs={{16,0},{17,1},{18,2},{19,3},{20,4},{21,5},{22,6},{23,7},{24,8},{25... | collective-permute-start | bytes 786440 | tf_op jit(solution)/shard_map/while/body/eval_jaxpr/ppermute | solution.py:17
  433.8 22.7 %copy-start.1 = (bf16[128,2048]{1,0:T(8,128)(2,1)}, bf16[128,2048]{1,0:T(8,128)(2,1)S(1)}, u32[]{:S(2)}) copy-start(bf16[128,2048]{1,0:T(8,128)(2,1)S(1)} %get-tuple-element.261) | copy-start | bytes 1572868
  433.8 29.6 %copy-start.3 = (bf16[128,2048]{1,0:T(8,128)(2,1)}, bf16[128,2048]{1,0:T(8,128)(2,1)S(1)}, u32[]{:S(2)}) copy-start(bf16[128,2048]{1,0:T(8,128)(2,1)S(1)} %get-tuple-element.259) | copy-start | bytes 1572868
  433.8 26.1 %all-gather.8.cloned.1.call-start = ((), (), s32[]{:S(2)}) async-start(), calls=%async_computation.2 | async-start | bytes 1572864 | tf_op jit(solution)/shard_map/all_gather | solution.py:95
  434.5 47.5 %all-gather.10.cloned.1.call-start = ((), (), s32[]{:S(2)}) async-start(), calls=%async_computation.3 | async-start | bytes 1572864 | tf_op jit(solution)/shard_map/all_gather | solution.py:96
Sparse Core Ops, SparseCore 0:
  9.5 102.6 all-gather.5
  117.0 18.4 all-reduce.2
  139.5 72.2 all-reduce.4
  225.6 16.1 all-reduce.2
  245.9 72.1 all-reduce.4
  332.0 16.1 all-reduce.2
  352.2 72.1 all-reduce.4
  436.1 23.6 all-gather.7
  462.0 19.9 all-gather.9
